TPU v7x, 32 devices: a whole 2x2x4 slice. The times are simulated.
32 devices in a mesh: groups: 2 (over y), seq: 8 (over z, x), tp: 2 (over core).
Axes of the slice: x: 2, y: 2, z: 4, core: 2. Of those that a mesh axis runs over, the one named last changes fastest.
Arguments:
- span_queries: bfloat16 [128, 64, 128], P(('groups', 'seq'), 'tp'), parts along dimension 0, may hold values from -180 to 180
- span_keys: bfloat16 [128, 4, 128], P(('groups', 'seq'), 'tp'), parts along dimension 0, may hold values from -9 to 9
- span_values: bfloat16 [128, 4, 128], P(('groups', 'seq'), 'tp'), parts along dimension 0, may hold values from -6.5 to 6.5
- prefix_keys: bfloat16 [1152, 4, 128], P(('groups', 'seq'), 'tp'), parts along dimension 0, may hold values from -9 to 9
- prefix_values: bfloat16 [1152, 4, 128], P(('groups', 'seq'), 'tp'), parts along dimension 0, may hold values from -6.5 to 6.5
- prefix_lengths: int32 [16], P('groups'), parts along dimension 0, may hold values from 1 to 72
- decode_queries: bfloat16 [32, 64, 128], P(('groups', 'seq'), 'tp'), parts along dimension 0, may hold values from -180 to 180
- decode_new_keys: bfloat16 [32, 4, 128], P(('groups', 'seq'), 'tp'), parts along dimension 0, may hold values from -6 to 6
- decode_new_values: bfloat16 [32, 4, 128], P(('groups', 'seq'), 'tp'), parts along dimension 0, may hold values from -6 to 6
- decode_key_cache: bfloat16 [64, 256, 4, 128], P(('groups', 'seq'), None, 'tp'), parts along dimension 0, may hold values from -6 to 6
- decode_value_cache: bfloat16 [64, 256, 4, 128], P(('groups', 'seq'), None, 'tp'), parts along dimension 0, may hold values from -6 to 6
- owner_map: int32 [32, 1], P('groups'), parts along dimension 0, may hold values from 0 to 7; in each aligned block of 16 rows (0 to 15, 16 to 31, ...) at most 4 rows name the same one
- decode_lengths: int32 [32], P('groups'), parts along dimension 0, may hold values from 1 to 256
Outputs:
- prefill_out: bfloat16 [128, 64, 128], P(('groups', 'seq'), 'tp'), parts along dimension 0
- decode_out: bfloat16 [64, 64, 128], P(('groups', 'seq'), 'tp'), parts along dimension 0
There are 2 independent parts, one for each index of `groups`. A program takes and returns all parts, laid end to end along the dimension named above; each array names one. Nothing has to cross between parts.
Inputs may be any that keep to these rules, and one draw needn't show every extreme that they name: `owner_map`: no shard owns more than 4 requests, and some shard owns exactly 4.
All inputs are finite; a program needn't handle non-finite values.
Results may differ from a plain program's by a relative error of at most 0.005.
Values may be sent and summed in bfloat16 or wider, within the bound.
No kernel may reach another device: no remote copies, remote signals or barrier semaphores. Data moves between devices by JAX's collectives and lax.ppermute only.
A program may use at most 64 MiB of HBM per device.

v0:
```python
import jax
import jax.numpy as jnp
from jax import lax
from jax.sharding import PartitionSpec as P

LOWEST = -1e30


def lookup_small(table, wanted):
    columns = jnp.arange(table.shape[0], dtype=jnp.int32)
    return jnp.sum(jnp.where(wanted[:, None] == columns[None, :], table[None, :], 0), axis=1)


def block_split(length):
    blocks = 1
    while length // blocks > 512 or length % blocks != 0:
        blocks += 1
    return blocks


def online_step(carried, queries, key_rows, value_rows, allowed):
    running_max, normalizer, weighted = carried
    scale = queries.shape[-1] ** (-0.5)
    scores = (
        jnp.einsum("tkgd,nkd->tkgn", queries, key_rows, preferred_element_type=jnp.float32) * scale
    )
    visible = allowed[:, None, None, :]
    scores = jnp.where(visible, scores, LOWEST)
    new_max = jnp.maximum(running_max, jnp.max(scores, axis=-1))
    weights = jnp.where(visible, jnp.exp(scores - new_max[..., None]), 0.0)
    factor = jnp.exp(running_max - new_max)
    normalizer = normalizer * factor + jnp.sum(weights, axis=-1)
    weighted = weighted * factor[..., None] + jnp.einsum(
        "tkgn,nkd->tkgd",
        weights.astype(jnp.bfloat16),
        value_rows,
        preferred_element_type=jnp.float32,
    )
    return (new_max, normalizer, weighted)


def guarded_step(carried, queries, key_rows, value_rows, allowed):
    return lax.cond(
        jnp.any(allowed),
        lambda inner: online_step(inner, queries, key_rows, value_rows, allowed),
        lambda inner: inner,
        carried,
    )


def fold_rows(carried, queries, key_rows, value_rows, allowed):
    length = key_rows.shape[0]
    blocks = block_split(length)
    if blocks == 1:
        return guarded_step(carried, queries, key_rows, value_rows, allowed)
    width = length // blocks
    stacked = (
        key_rows.reshape((blocks, width) + key_rows.shape[1:]),
        value_rows.reshape((blocks, width) + value_rows.shape[1:]),
        allowed.reshape(allowed.shape[0], blocks, width).transpose(1, 0, 2),
    )

    def visit(inner_carry, parts):
        return (guarded_step(inner_carry, queries, parts[0], parts[1], parts[2]), None)

    carried, unused = lax.scan(visit, carried, stacked)
    return carried


def on_device(
    span_queries,
    span_keys,
    span_values,
    prefix_keys,
    prefix_values,
    prefix_lengths,
    decode_queries,
    decode_new_keys,
    decode_new_values,
    decode_key_cache,
    decode_value_cache,
    owner_map,
    decode_lengths,
):
    device = lax.axis_index("seq")
    tokens_here, heads_here, head_dim = span_queries.shape
    kv_here = span_keys.shape[1]
    group_size = heads_here // kv_here
    queries = span_queries.reshape(tokens_here, kv_here, group_size, head_dim)
    token_index = device * tokens_here + jnp.arange(tokens_here, dtype=jnp.int32)
    prefix_here = prefix_keys.shape[0]
    initial = (
        jnp.full((tokens_here, kv_here, group_size), LOWEST, jnp.float32),
        jnp.zeros((tokens_here, kv_here, group_size), jnp.float32),
        jnp.zeros((tokens_here, kv_here, group_size, head_dim), jnp.float32),
    )
    stride = prefix_here + tokens_here
    both_keys = jnp.concatenate([prefix_keys, span_keys], axis=0)
    both_values = jnp.concatenate([prefix_values, span_values], axis=0)
    carried = initial
    key_rows = lax.all_gather(both_keys, "seq", axis=0, tiled=True)
    value_rows = lax.all_gather(both_values, "seq", axis=0, tiled=True)
    length = key_rows.shape[0]
    shards = length // stride
    tail = key_rows.shape[1:]
    keys_split = key_rows.reshape((shards, stride) + tail)
    values_split = value_rows.reshape((shards, stride) + tail)
    prefix_k = keys_split[:, :prefix_here].reshape((shards * prefix_here,) + tail)
    prefix_v = values_split[:, :prefix_here].reshape((shards * prefix_here,) + tail)
    span_k = keys_split[:, prefix_here:].reshape((shards * tokens_here,) + tail)
    span_v = values_split[:, prefix_here:].reshape((shards * tokens_here,) + tail)
    prefix_position = jnp.arange(shards * prefix_here, dtype=jnp.int32)
    prefix_ok = prefix_position % prefix_here < lookup_small(
        prefix_lengths, prefix_position // prefix_here
    )
    carried = fold_rows(
        carried,
        queries,
        prefix_k,
        prefix_v,
        jnp.broadcast_to(prefix_ok[None, :], (tokens_here, prefix_k.shape[0])),
    )
    span_position = jnp.arange(shards * tokens_here, dtype=jnp.int32)
    carried = fold_rows(
        carried, queries, span_k, span_v, span_position[None, :] <= token_index[:, None]
    )
    running_max, normalizer, weighted = carried
    prefill_out = (
        (weighted / normalizer[..., None])
        .reshape(tokens_here, heads_here, head_dim)
        .astype(jnp.bfloat16)
    )
    owners = owner_map[:, 0]
    requests = owners.shape[0]
    order = jnp.arange(requests, dtype=jnp.int32)
    earlier = (owners[None, :] == owners[:, None]) & (order[None, :] < order[:, None])
    ranking = jnp.sum(earlier.astype(jnp.int32), axis=1)
    slots_here = decode_key_cache.shape[0]
    slot_ids = jnp.arange(slots_here, dtype=jnp.int32)
    query_rows = lax.all_gather(decode_queries, "seq", axis=0, tiled=True)
    new_keys = lax.all_gather(decode_new_keys, "seq", axis=0, tiled=True)
    new_values = lax.all_gather(decode_new_values, "seq", axis=0, tiled=True)
    chosen = (owners == device)[None, :] & (ranking[None, :] == slot_ids[:, None])
    selector = chosen.astype(jnp.bfloat16)
    picked_queries = jnp.einsum(
        "sn,nhd->shd", selector, query_rows, preferred_element_type=jnp.float32
    )
    picked_keys = jnp.einsum("sn,nkd->skd", selector, new_keys, preferred_element_type=jnp.float32)
    picked_values = jnp.einsum(
        "sn,nkd->skd", selector, new_values, preferred_element_type=jnp.float32
    )
    picked_lengths = jnp.sum(jnp.where(chosen, decode_lengths[None, :], 0), axis=1)
    context = decode_key_cache.shape[1]
    grouped = picked_queries.astype(jnp.bfloat16).reshape(slots_here, kv_here, group_size, head_dim)
    own_keys = picked_keys.astype(jnp.bfloat16)
    own_values = picked_values.astype(jnp.bfloat16)
    scale = head_dim ** (-0.5)
    scores = (
        jnp.einsum("skgd,sckd->skgc", grouped, decode_key_cache, preferred_element_type=jnp.float32)
        * scale
    )
    visible = (jnp.arange(context, dtype=jnp.int32)[None, :] < picked_lengths[:, None])[
        :, None, None, :
    ]
    scores = jnp.where(visible, scores, LOWEST)
    own_score = (
        jnp.einsum("skgd,skd->skg", grouped, own_keys, preferred_element_type=jnp.float32) * scale
    )
    top_score = jnp.maximum(jnp.max(scores, axis=-1), own_score)
    weights = jnp.where(visible, jnp.exp(scores - top_score[..., None]), 0.0)
    own_weight = jnp.exp(own_score - top_score)
    total_weight = jnp.sum(weights, axis=-1) + own_weight
    rounded_own = lax.optimization_barrier(own_weight.astype(jnp.bfloat16)).astype(jnp.float32)
    mixed = jnp.einsum(
        "skgc,sckd->skgd",
        weights.astype(jnp.bfloat16),
        decode_value_cache,
        preferred_element_type=jnp.float32,
    )
    mixed = mixed + rounded_own[..., None] * own_values.astype(jnp.float32)[:, :, None, :]
    count_here = jnp.sum((owners == device).astype(jnp.int32))
    used = (slot_ids < count_here)[:, None, None, None]
    decode_out = (
        jnp.where(used, mixed / total_weight[..., None], 0.0)
        .reshape(slots_here, heads_here, head_dim)
        .astype(jnp.bfloat16)
    )
    return (prefill_out, decode_out)


def solution(mesh):
    return jax.shard_map(
        on_device,
        mesh=mesh,
        in_specs=(
            P(("groups", "seq"), "tp", None),
            P(("groups", "seq"), "tp", None),
            P(("groups", "seq"), "tp", None),
            P(("groups", "seq"), "tp", None),
            P(("groups", "seq"), "tp", None),
            P("groups"),
            P(("groups", "seq"), "tp", None),
            P(("groups", "seq"), "tp", None),
            P(("groups", "seq"), "tp", None),
            P(("groups", "seq"), None, "tp", None),
            P(("groups", "seq"), None, "tp", None),
            P("groups", None),
            P("groups"),
        ),
        out_specs=(P(("groups", "seq"), "tp", None), P(("groups", "seq"), "tp", None)),
        check_vma=False,
    )
```

profile of v0, /device:TPU:0, one launch (start us, length us, event | category | flops | bytes accessed | tf_op | source)
XLA Modules:
  0.0 148.8 jit_solution(11207647977653412298)
XLA Ops:
  0.7 0.7 iota_compare_fusion.3
  2.0 0.7 select_reduce_fusion
  2.9 0.7 copy-done.5
  3.6 32.7 %all_gather.15 = bf16[640,2,128]{2,1,0:T(2,128)(2,1)S(1)} all-gather(bf16[80,2,128]{2,1,0:T(2,128)(2,1)S(1)} %pad_maximum_fusion), channel_id=1, replica_groups=mesh['groups'=2,'seq'=8,'tp'=2] {'seq'}, dimensions={0}, use_global_device_ids=true | all-gather | bytes 368640 | tf_op jit(solution)/shard_map/all_gather | solution.py:101
  36.4 0.8 copy-done.1
  37.2 0.8 copy-done.3
  38.1 30.9 %all_gather.16 = bf16[640,2,128]{2,1,0:T(2,128)(2,1)S(1)} all-gather(bf16[80,2,128]{2,1,0:T(2,128)(2,1)S(1)} %pad_maximum_fusion.1), channel_id=1, replica_groups=mesh['groups'=2,'seq'=8,'tp'=2] {'seq'}, dimensions={0}, use_global_device_ids=true | all-gather | bytes 368640 | tf_op jit(solution)/shard_map/all_gather | solution.py:102
  69.1 4.4 %while.14 = (s32[]{:T(128)}, f32[8,2,16]{2,0,1:T(8,128)S(1)}, f32[8,2,16]{2,0,1:T(8,128)S(1)}, f32[8,2,16,128]{3,2,0,1:T(8,128)S(1)}, pred[2,8,288]{2,1,0:T(8,12...) while((s32[]{:T(128)}, f32[8,2,16]{2,0,1:T(8,128)S(1)}, ...), condition=%wide.region_8.9_spmd, body=%wide.region_2.8_spmd.sunk | while | flops 38480640 | bytes 1649647 | solution.py:66
  69.2 0.7 fusion.72
  70.5 0.9 conditional.4
  70.5 0.3 fusion.67
  70.8 0.2 fusion.4
  71.1 0.3 fusion.2
  71.4 0.7 fusion.72
  72.7 0.9 conditional.4
  72.7 0.3 fusion.67
  73.3 0.3 fusion.2
  73.6 0.7 conditional.2
  73.6 0.3 fusion.68
  74.1 0.2 fusion.16
  74.5 0.6 copy.71
  75.2 30.5 %all_gather.17 = bf16[16,32,128]{2,1,0:T(8,128)(2,1)S(1)} all-gather(bf16[2,32,128]{2,1,0:T(8,128)(2,1)S(1)} %copy-done.4), channel_id=1, replica_groups=mesh['groups'=2,'seq'=8,'tp'=2] {'seq'}, dimensions={0}, use_global_device_ids=true | all-gather | bytes 147456 | tf_op jit(solution)/shard_map/all_gather | solution.py:140
  105.7 0.7 copy-done.10
  106.5 0.6 convert_reduce_fusion.1
  107.2 0.7 copy-done.9
  108.2 0.3 fusion.69
  108.5 0.7 copy-done.7
  109.2 20.5 %all_gather.18 = bf16[16,2,128]{2,1,0:T(2,128)(2,1)S(1)} all-gather(bf16[2,2,128]{2,1,0:T(2,128)(2,1)S(1)} %copy-done.7), channel_id=1, replica_groups=mesh['groups'=2,'seq'=8,'tp'=2] {'seq'}, dimensions={0}, use_global_device_ids=true | all-gather | bytes 9216 | tf_op jit(solution)/shard_map/all_gather | solution.py:141
  130.2 0.7 copy-done.8
  130.8 16.3 %all_gather.19 = bf16[16,2,128]{2,1,0:T(2,128)(2,1)S(1)} all-gather(bf16[2,2,128]{2,1,0:T(2,128)(2,1)S(1)} %copy-done.8), channel_id=1, replica_groups=mesh['groups'=2,'seq'=8,'tp'=2] {'seq'}, dimensions={0}, use_global_device_ids=true | all-gather | bytes 9216 | tf_op jit(solution)/shard_map/all_gather | solution.py:142
  147.2 0.6 iota_compare_fusion.5
  147.9 0.9 fusion.34
  (57 shorter events, 2.2 us)
Async XLA Ops:
  0.6 107.6 %copy-start = (bf16[4,256,2,128]{3,2,1,0:T(2,128)(2,1)S(1)}, bf16[4,256,2,128]{3,2,1,0:T(2,128)(2,1)}, u32[]{:S(2)}) copy-start(bf16[4,256,2,128]{3,2,1,0:T(2,128)(2,1)} %param.28) | copy-start | bytes 1572868
  0.6 2.3 %copy-start.2 = (bf16[72,2,128]{2,1,0:T(2,128)(2,1)S(1)}, bf16[72,2,128]{2,1,0:T(2,128)(2,1)}, u32[]{:S(2)}) copy-start(bf16[72,2,128]{2,1,0:T(2,128)(2,1)} %param.22) | copy-start | bytes 110596
  2.9 0.7 copy-start.5
  36.4 0.8 copy-start.1
  37.2 0.8 copy-start.3
  37.2 0.8 copy-start.6
  74.5 0.7 copy-start.4
  105.7 0.7 copy-start.10
  107.2 0.7 copy-start.9
  108.1 39.8 %copy-start.11 = (bf16[4,256,2,128]{3,2,1,0:T(2,128)(2,1)S(1)}, bf16[4,256,2,128]{3,2,1,0:T(2,128)(2,1)}, u32[]{:S(2)}) copy-start(bf16[4,256,2,128]{3,2,1,0:T(2,128)(2,1)} %param.29) | copy-start | bytes 1572868
  108.5 0.7 copy-start.7
  130.1 0.7 copy-start.8
where the time goes:
time: 149 us
  blocking collectives  131 us (88%)
  local copies, waits for them, and re-layouts  5.93 us (4%)
  other arithmetic  5.57 us (4%)
  matrix products  3.39 us (2%)
  between operations  1.53 us (1%)
  loops' own time  1.5 us (1%)
    all_gather x1, blocking collectives, on_device(): key_rows = lax.all_gather(both_keys, 'seq', axis=0, tiled=True)  32.7 us
    all_gather x1, blocking collectives, on_device(): value_rows = lax.all_gather(both_values, 'seq', axis=0, tiled=True)  30.9 us
    all_gather x1, blocking collectives, on_device(): query_rows = lax.all_gather(decode_queries, 'seq', axis=0, tiled=True)  30.5 us
    all_gather x1, blocking collectives, on_device(): new_keys = lax.all_gather(decode_new_keys, 'seq', axis=0, tiled=True)  20.5 us
    all_gather x1, blocking collectives, on_device(): new_values = lax.all_gather(decode_new_values, 'seq', axis=0, tiled=True)  16.3 us
    unnamed x24, local copies, waits for them, and re-layouts  4.99 us

commit v1 on v0

--- a/solution.py
+++ b/solution.py
@@ -137,14 +137,42 @@
     ranking = jnp.sum(earlier.astype(jnp.int32), axis=1)
     slots_here = decode_key_cache.shape[0]
     slot_ids = jnp.arange(slots_here, dtype=jnp.int32)
-    query_rows = lax.all_gather(decode_queries, "seq", axis=0, tiled=True)
     new_keys = lax.all_gather(decode_new_keys, "seq", axis=0, tiled=True)
     new_values = lax.all_gather(decode_new_values, "seq", axis=0, tiled=True)
     chosen = (owners == device)[None, :] & (ranking[None, :] == slot_ids[:, None])
     selector = chosen.astype(jnp.bfloat16)
-    picked_queries = jnp.einsum(
-        "sn,nhd->shd", selector, query_rows, preferred_element_type=jnp.float32
-    )
+    size, place, span = (lax.axis_size("seq"), lax.axis_index("seq"), decode_queries.shape[0])
+    right = [(i, (i + 1) % size) for i in range(size)]
+    left = [(i, (i - 1) % size) for i in range(size)]
+    halfway = size // 2
+    from_left = from_right = decode_queries
+    running = jnp.einsum(
+        "sn,nhd->shd",
+        lax.dynamic_slice_in_dim(selector, place * span, decode_queries.shape[0], axis=1),
+        decode_queries,
+        preferred_element_type=jnp.float32,
+    )
+    for step in range(1, halfway + 1):
+        from_left = lax.ppermute(from_left, "seq", right)
+        if step < size - halfway:
+            from_right = lax.ppermute(from_right, "seq", left)
+            running = running + jnp.einsum(
+                "sn,nhd->shd",
+                lax.dynamic_slice_in_dim(
+                    selector, (place + step) % size * span, from_right.shape[0], axis=1
+                ),
+                from_right,
+                preferred_element_type=jnp.float32,
+            )
+        running = running + jnp.einsum(
+            "sn,nhd->shd",
+            lax.dynamic_slice_in_dim(
+                selector, (place - step) % size * span, from_left.shape[0], axis=1
+            ),
+            from_left,
+            preferred_element_type=jnp.float32,
+        )
+    picked_queries = running
     picked_keys = jnp.einsum("sn,nkd->skd", selector, new_keys, preferred_element_type=jnp.float32)
     picked_values = jnp.einsum(
         "sn,nkd->skd", selector, new_values, preferred_element_type=jnp.float32

time: 149 us -> 141 us (0.946)
  blocking collectives: 131 us -> 96.3 us
  starting transfers between devices: 0 us -> 15.6 us
  waiting for transfers between devices: 0 us -> 8.49 us
  matrix products: 3.39 us -> 5.24 us
    all_gather x1 -> x0, blocking collectives: 30.5 us -> none  [on_device(): query_rows = lax.all_gather(decode_queries, 'seq', axis=0, tiled=True)]
    ppermute x0 -> x7, starting transfers between devices: none -> 15.6 us  [the longest x3 10.6 us: on_device(): from_right = lax.ppermute(from_right, 'seq', left)]
    ppermute x0 -> x7, waiting for transfers between devices: none -> 8.49 us  [the longest x4 8.48 us: on_device(): from_left = lax.ppermute(from_left, 'seq', right)]
    all_gather x1, blocking collectives: 20.5 us -> 18.2 us  [on_device(): new_keys = lax.all_gather(decode_new_keys, 'seq', axis=0, tiled=True)]
    all_gather x1, blocking collectives: 32.7 us -> 30.9 us  [on_device(): key_rows = lax.all_gather(both_keys, 'seq', axis=0, tiled=True)]
    dot_general x1 -> x8, matrix products: 0.16 us -> 1.73 us  [the longest x4 0.86 us: on_device(): jnp.einsum('sn,nhd->shd', lax.dynamic_slice_in_dim(selector, (place - ste...]
    unnamed x24 -> x27, local copies, waits for them, and re-layouts: 4.99 us -> 5.89 us
  transfers between devices with their start and end apart: 0 -> 7, of which waited for: 0 -> 3; matrix products, arithmetic and copies ran while one was open for 0% -> 7% of each run, Pallas kernels for 0% -> 0%
where the time goes in v1:
time: 141 us
  blocking collectives  96.3 us (68%)
  starting transfers between devices  15.6 us (11%)
  waiting for transfers between devices  8.49 us (6%)
  local copies, waits for them, and re-layouts  6.82 us (5%)
  matrix products  5.24 us (4%)
  other arithmetic  5.04 us (4%)
  between operations  1.67 us (1%)
  loops' own time  1.48 us (1%)
    all_gather x1, blocking collectives, on_device(): key_rows = lax.all_gather(both_keys, 'seq', axis=0, tiled=True)  30.9 us
    all_gather x1, blocking collectives, on_device(): value_rows = lax.all_gather(both_values, 'seq', axis=0, tiled=True)  30.9 us
    all_gather x1, blocking collectives, on_device(): new_keys = lax.all_gather(decode_new_keys, 'seq', axis=0, tiled=True)  18.2 us
    all_gather x1, blocking collectives, on_device(): new_values = lax.all_gather(decode_new_values, 'seq', axis=0, tiled=True)  16.3 us
    ppermute x3, starting transfers between devices, on_device(): from_right = lax.ppermute(from_right, 'seq', left)  10.6 us
    ppermute x4, waiting for transfers between devices, on_device(): from_left = lax.ppermute(from_left, 'seq', right)  8.48 us
    unnamed x27, local copies, waits for them, and re-layouts  5.89 us
    ppermute x4, starting transfers between devices, on_device(): from_left = lax.ppermute(from_left, 'seq', right)  4.98 us
  transfers between devices with their start and end apart: 7, of which 3 were waited for; matrix products, arithmetic and copies ran while one was open for 7% of the time, Pallas kernels for 0%

profile of v1, /device:TPU:0, one launch (start us, length us, event | category | flops | bytes accessed | tf_op | source)
XLA Modules:
  0.0 140.6 jit_solution(13253546935683407031)
XLA Ops:
  0.7 0.8 copy.86
  1.5 3.0 %collective-permute-start.1 = (bf16[2,32,128]{2,0,1:T(2,128)(2,1)S(1)}, bf16[2,32,128]{2,0,1:T(2,128)(2,1)S(1)}, u32[]{:S(2)}, u32[]{:S(2)}) collective-permute-start(bf16[2,32,128]{2,0,1:T(2,128)(2,1)S(1)} %copy.86), channel_id=1, source_target_pairs={{0,2},{2,4},{4,6},{6,8},{8,10},{10,12},{12,14},{14,0},{1,3},{3,5},... | collective-permute-start | bytes 49160 | tf_op jit(solution)/shard_map/ppermute | solution.py:156
  4.5 3.1 %collective-permute-start = (bf16[2,32,128]{2,0,1:T(2,128)(2,1)S(1)}, bf16[2,32,128]{2,0,1:T(2,128)(2,1)S(1)}, u32[]{:S(2)}, u32[]{:S(2)}) collective-permute-start(bf16[2,32,128]{2,0,1:T(2,128)(2,1)S(1)} %copy.86), channel_id=1, source_target_pairs={{0,14},{2,0},{4,2},{6,4},{8,6},{10,8},{12,10},{14,12},{1,15},{3,1}... | collective-permute-start | bytes 49160 | tf_op jit(solution)/shard_map/ppermute | solution.py:158
  7.6 0.7 iota_compare_fusion.4
  9.0 0.6 copy-done.9
  9.8 0.7 copy-done.5
  10.5 30.9 %all_gather.12 = bf16[640,2,128]{2,1,0:T(2,128)(2,1)S(1)} all-gather(bf16[80,2,128]{2,1,0:T(2,128)(2,1)S(1)} %pad_maximum_fusion), channel_id=1, replica_groups=mesh['groups'=2,'seq'=8,'tp'=2] {'seq'}, dimensions={0}, use_global_device_ids=true | all-gather | bytes 368640 | tf_op jit(solution)/shard_map/all_gather | solution.py:101
  41.5 0.8 copy-done.1
  42.3 0.8 copy-done.4
  43.1 30.9 %all_gather.13 = bf16[640,2,128]{2,1,0:T(2,128)(2,1)S(1)} all-gather(bf16[80,2,128]{2,1,0:T(2,128)(2,1)S(1)} %pad_maximum_fusion.1), channel_id=1, replica_groups=mesh['groups'=2,'seq'=8,'tp'=2] {'seq'}, dimensions={0}, use_global_device_ids=true | all-gather | bytes 368640 | tf_op jit(solution)/shard_map/all_gather | solution.py:102
  74.2 4.5 %while.14 = (s32[]{:T(128)}, f32[8,2,16]{2,0,1:T(8,128)S(1)}, f32[8,2,16]{2,0,1:T(8,128)S(1)}, f32[8,2,16,128]{3,2,0,1:T(8,128)S(1)}, pred[2,8,288]{2,1,0:T(8,12...) while((s32[]{:T(128)}, f32[8,2,16]{2,0,1:T(8,128)S(1)}, ...), condition=%wide.region_8.9_spmd, body=%wide.region_2.8_spmd.sunk | while | flops 38480640 | bytes 1649647 | solution.py:66
  74.2 0.7 fusion.101
  75.5 0.9 conditional.4
  76.4 0.7 fusion.101
  77.8 0.9 conditional.4
  78.7 0.6 convert_reduce_fusion.1
  79.6 0.6 copy-done.11
  80.3 0.6 copy-done.7
  80.9 18.2 %all_gather.14 = bf16[16,2,128]{2,1,0:T(2,128)(2,1)S(1)} all-gather(bf16[2,2,128]{2,1,0:T(2,128)(2,1)S(1)} %copy-done.7), channel_id=1, replica_groups=mesh['groups'=2,'seq'=8,'tp'=2] {'seq'}, dimensions={0}, use_global_device_ids=true | all-gather | bytes 9216 | tf_op jit(solution)/shard_map/all_gather | solution.py:140
  99.4 0.4 copy-done.8
  99.8 16.3 %all_gather.15 = bf16[16,2,128]{2,1,0:T(2,128)(2,1)S(1)} all-gather(bf16[2,2,128]{2,1,0:T(2,128)(2,1)S(1)} %copy-done.8), channel_id=1, replica_groups=mesh['groups'=2,'seq'=8,'tp'=2] {'seq'}, dimensions={0}, use_global_device_ids=true | all-gather | bytes 9216 | tf_op jit(solution)/shard_map/all_gather | solution.py:141
  116.4 0.7 conditional.2
  117.3 0.6 copy-done.2
  118.1 0.7 iota_compare_fusion.5
  118.9 0.6 copy.85
  119.5 2.0 %collective-permute-start.3 = (bf16[2,32,128]{2,0,1:T(2,128)(2,1)S(1)}, bf16[2,32,128]{2,0,1:T(2,128)(2,1)S(1)}, u32[]{:S(2)}, u32[]{:S(2)}) collective-permute-start(bf16[2,32,128]{2,0,1:T(2,128)(2,1)S(1)} %collective-permute-done.1), channel_id=1, source_target_pairs={{0,2},{2,4},{4,6},{6,8},{8,10},{10,12},{12,14},{14,0},{1,3},{3,5},... | collective-permute-start | bytes 49160 | tf_op jit(solution)/shard_map/ppermute | solution.py:156
  121.5 2.8 %collective-permute-start.2 = (bf16[2,32,128]{2,0,1:T(2,128)(2,1)S(1)}, bf16[2,32,128]{2,0,1:T(2,128)(2,1)S(1)}, u32[]{:S(2)}, u32[]{:S(2)}) collective-permute-start(bf16[2,32,128]{2,0,1:T(2,128)(2,1)S(1)} %collective-permute-done), channel_id=1, source_target_pairs={{0,14},{2,0},{4,2},{6,4},{8,6},{10,8},{12,10},{14,12},{1,15},{3,1}... | collective-permute-start | bytes 49160 | tf_op jit(solution)/shard_map/ppermute | solution.py:158
  124.7 1.3 collective-permute-done.3
  126.2 4.8 %collective-permute-start.4 = (bf16[2,32,128]{2,0,1:T(2,128)(2,1)S(1)}, bf16[2,32,128]{2,0,1:T(2,128)(2,1)S(1)}, u32[]{:S(2)}, u32[]{:S(2)}) collective-permute-start(bf16[2,32,128]{2,0,1:T(2,128)(2,1)S(1)} %collective-permute-done.2), channel_id=1, source_target_pairs={{0,14},{2,0},{4,2},{6,4},{8,6},{10,8},{12,10},{14,12},{1,15},{3,1}... | collective-permute-start | bytes 49160 | tf_op jit(solution)/shard_map/ppermute | solution.py:158
  131.2 1.2 collective-permute-done.5
  132.8 6.0 %collective-permute-done.6 = bf16[2,32,128]{2,0,1:T(2,128)(2,1)S(1)} collective-permute-done((bf16[2,32,128]{2,0,1:T(2,128)(2,1)S(1)}, bf16[2,32,128]{2,0,1:T(2,128)(2,1)S(1)}, u32[]{:S(2)}, u32[]{:S(2)}) %collective-permute-start.6) | collective-permute-done | bytes 16416 | tf_op jit(solution)/shard_map/ppermute | solution.py:156
  139.8 0.9 fusion.36
  (81 shorter events, 6.4 us)
Async XLA Ops:
  0.6 138.6 %copy-start = (bf16[4,256,2,128]{3,2,1,0:T(2,128)(2,1)S(1)}, bf16[4,256,2,128]{3,2,1,0:T(2,128)(2,1)}, u32[]{:S(2)}) copy-start(bf16[4,256,2,128]{3,2,1,0:T(2,128)(2,1)} %param.28) | copy-start | bytes 1572868
  0.6 9.2 %copy-start.3 = (bf16[72,2,128]{2,1,0:T(2,128)(2,1)S(1)}, bf16[72,2,128]{2,1,0:T(2,128)(2,1)}, u32[]{:S(2)}) copy-start(bf16[72,2,128]{2,1,0:T(2,128)(2,1)} %param.22) | copy-start | bytes 110596
  1.5 118.1 %collective-permute-start.1 = (bf16[2,32,128]{2,0,1:T(2,128)(2,1)S(1)}, bf16[2,32,128]{2,0,1:T(2,128)(2,1)S(1)}, u32[]{:S(2)}, u32[]{:S(2)}) collective-permute-start(bf16[2,32,128]{2,0,1:T(2,128)(2,1)S(1)} %copy.86), channel_id=1, source_target_pairs={{0,2},{2,4},{4,6},{6,8},{8,10},{10,12},{12,14},{14,0},{1,3},{3,5},... | collective-permute-start | bytes 49160 | tf_op jit(solution)/shard_map/ppermute | solution.py:156
  4.5 117.0 %collective-permute-start = (bf16[2,32,128]{2,0,1:T(2,128)(2,1)S(1)}, bf16[2,32,128]{2,0,1:T(2,128)(2,1)S(1)}, u32[]{:S(2)}, u32[]{:S(2)}) collective-permute-start(bf16[2,32,128]{2,0,1:T(2,128)(2,1)S(1)} %copy.86), channel_id=1, source_target_pairs={{0,14},{2,0},{4,2},{6,4},{8,6},{10,8},{12,10},{14,12},{1,15},{3,1}... | collective-permute-start | bytes 49160 | tf_op jit(solution)/shard_map/ppermute | solution.py:158
  8.9 0.7 copy-start.9
  9.8 0.7 copy-start.5
  41.5 0.8 copy-start.1
  42.3 0.8 copy-start.4
  42.3 0.8 copy-start.6
  74.2 4.5 %copy-start.10 = (s32[16,1]{0,1:T(1,128)S(1)}, s32[16,1]{0,1:T(1,128)}, u32[]{:S(2)}) copy-start(s32[16,1]{0,1:T(1,128)} %param.30) | copy-start | bytes 196
  79.5 0.7 copy-start.11
  80.3 0.7 copy-start.7
  99.2 0.7 copy-start.8
  117.2 0.7 copy-start.2
  119.5 6.4 %collective-permute-start.3 = (bf16[2,32,128]{2,0,1:T(2,128)(2,1)S(1)}, bf16[2,32,128]{2,0,1:T(2,128)(2,1)S(1)}, u32[]{:S(2)}, u32[]{:S(2)}) collective-permute-start(bf16[2,32,128]{2,0,1:T(2,128)(2,1)S(1)} %collective-permute-done.1), channel_id=1, source_target_pairs={{0,2},{2,4},{4,6},{6,8},{8,10},{10,12},{12,14},{14,0},{1,3},{3,5},... | collective-permute-start | bytes 49160 | tf_op jit(solution)/shard_map/ppermute | solution.py:156
  121.5 4.7 %collective-permute-start.2 = (bf16[2,32,128]{2,0,1:T(2,128)(2,1)S(1)}, bf16[2,32,128]{2,0,1:T(2,128)(2,1)S(1)}, u32[]{:S(2)}, u32[]{:S(2)}) collective-permute-start(bf16[2,32,128]{2,0,1:T(2,128)(2,1)S(1)} %collective-permute-done), channel_id=1, source_target_pairs={{0,14},{2,0},{4,2},{6,4},{8,6},{10,8},{12,10},{14,12},{1,15},{3,1}... | collective-permute-start | bytes 49160 | tf_op jit(solution)/shard_map/ppermute | solution.py:158
  126.0 6.4 %collective-permute-start.5 = (bf16[2,32,128]{2,0,1:T(2,128)(2,1)S(1)}, bf16[2,32,128]{2,0,1:T(2,128)(2,1)S(1)}, u32[]{:S(2)}, u32[]{:S(2)}) collective-permute-start(bf16[2,32,128]{2,0,1:T(2,128)(2,1)S(1)} %collective-permute-done.3), channel_id=1, source_target_pairs={{0,2},{2,4},{4,6},{6,8},{8,10},{10,12},{12,14},{14,0},{1,3},{3,5},... | collective-permute-start | bytes 49160 | tf_op jit(solution)/shard_map/ppermute | solution.py:156
  126.2 6.4 %collective-permute-start.4 = (bf16[2,32,128]{2,0,1:T(2,128)(2,1)S(1)}, bf16[2,32,128]{2,0,1:T(2,128)(2,1)S(1)}, u32[]{:S(2)}, u32[]{:S(2)}) collective-permute-start(bf16[2,32,128]{2,0,1:T(2,128)(2,1)S(1)} %collective-permute-done.2), channel_id=1, source_target_pairs={{0,14},{2,0},{4,2},{6,4},{8,6},{10,8},{12,10},{14,12},{1,15},{3,1}... | collective-permute-start | bytes 49160 | tf_op jit(solution)/shard_map/ppermute | solution.py:158
  132.4 6.4 %collective-permute-start.6 = (bf16[2,32,128]{2,0,1:T(2,128)(2,1)S(1)}, bf16[2,32,128]{2,0,1:T(2,128)(2,1)S(1)}, u32[]{:S(2)}, u32[]{:S(2)}) collective-permute-start(bf16[2,32,128]{2,0,1:T(2,128)(2,1)S(1)} %collective-permute-done.5), channel_id=1, source_target_pairs={{0,2},{2,4},{4,6},{6,8},{8,10},{10,12},{12,14},{14,0},{1,3},{3,5},... | collective-permute-start | bytes 49160 | tf_op jit(solution)/shard_map/ppermute | solution.py:156
  132.8 6.9 %copy-start.12 = (bf16[4,256,2,128]{3,2,1,0:T(2,128)(2,1)S(1)}, bf16[4,256,2,128]{3,2,1,0:T(2,128)(2,1)}, u32[]{:S(2)}) copy-start(bf16[4,256,2,128]{3,2,1,0:T(2,128)(2,1)} %param.29) | copy-start | bytes 1572868
